TPU v7x, 32 devices: a whole 2x2x4 slice. The times are simulated.
32 devices in a mesh: ta: 2 (over x), gz: 4 (over y, core), gy: 4 (over z).
Axes of the slice: x: 2, y: 2, z: 4, core: 2. Of those that a mesh axis runs over, the one named last changes fastest.
Arguments:
- propagator: bfloat16 [2, 4, 3, 12, 2, 4, 512], P(None, None, None, None, 'ta', 'gz', 'gy'), may hold values from -6 to 6
- links: bfloat16 [2, 3, 3, 2, 4, 512], P(None, None, None, 'ta', 'gz', 'gy'), may hold values from -2.5 to 2.5
- source_z: int32 [2, 4], replicated, may hold values from 0 to 3
- displacements: int32 [3], replicated, may hold values from 0 to 2, each once
- momenta: int32 [4], replicated, may hold values from 1 to 3
- gamma_perm: int32 [4, 4], replicated, may hold values from 0 to 3, each once within a row
- gamma_phase: int32 [4, 4], replicated, may hold values from 0 to 3
Outputs:
- correlator: float32 [2, 3, 4, 4, 2], replicated
Inputs may be any that keep to these rules, and one draw needn't show every extreme that they name: `displacements`: every displacement from -1 to 1 appears exactly once. `gamma_perm`: each row is a permutation of the four spin indices.
All inputs are finite; a program needn't handle non-finite values.
Results may differ from a plain program's by a relative error of at most 0.0003.
Values may be sent and summed in bfloat16 or wider, within the bound.
A program may use at most 64 MiB of HBM per device.

v0:
```python
import functools
import math

import jax
import jax.numpy as jnp
from jax import lax
from jax.experimental import pallas as pl
from jax.experimental.pallas import tpu as pltpu
from jax.sharding import PartitionSpec as P

MESH = pl.DeviceIdType.MESH
LANES = 128


def weights(lane_row, sizes, smem, place, scaling):
    ndisp, ng, np_, nz = sizes
    src, disp, mom, perm, phase = smem
    slice_at, depth_at = place
    nsteps = (ndisp - 1) // 2
    shape = (32, LANES)
    lane = lax.broadcasted_iota(jnp.int32, shape, 1) + lane_row * LANES
    row = lax.broadcasted_iota(jnp.int32, shape, 0)
    momentum = lane & (np_ - 1)
    out_part = (lane // np_) & 1
    gamma = (lane // (2 * np_)) & (ng - 1)
    entry = lane // (2 * np_ * ng)
    in_part = row // 16
    first = (row // 4) & 3
    second = row & 3
    reach = jnp.full(shape, 2 * nsteps + 1, jnp.int32)
    for j in range(ndisp):
        reach = jnp.where(entry == j, disp[j] - nsteps, reach)
    backward = reach < 0
    momenta = jnp.zeros(shape, jnp.int32)
    source = jnp.zeros(shape, jnp.int32)
    for p in range(np_):
        momenta = jnp.where(momentum == p, mom[p], momenta)
        source = jnp.where(momentum == p, src[slice_at, p], source)
    depth = depth_at - jnp.where(backward, reach, 0)
    turns = (momenta * (depth - source)).astype(jnp.float32) * (1.0 / nz)
    angle = (turns - jnp.floor(turns)) * (2.0 * math.pi)
    cosine = jnp.cos(angle)
    sine = jnp.sin(angle)
    sink = jnp.where(backward, second, first)
    other = jnp.where(backward, first, second)
    column = jnp.zeros(shape, jnp.int32)
    power = jnp.zeros(shape, jnp.int32)
    for g in range(ng):
        for s in range(4):
            here = (gamma == g) & (sink == s)
            column = jnp.where(here, perm[g, s], column)
            power = jnp.where(here, phase[g, s], power)
    quarter = power - out_part + jnp.where(backward, -in_part, in_part)
    quarter = quarter & 3
    value = jnp.where((quarter & 1) == 0, cosine, sine)
    value = jnp.where(quarter >= 2, -value, value)
    value = jnp.where((column == other) & (entry < ndisp), value * scaling, 0.0)
    return value, jnp.abs(reach)


def add_pairs(sums, left, turned, right, start, size):
    def rows(ref, s):
        return ref[pl.ds(start + s, size // 4, stride=4), :].reshape(-1, 8, LANES)

    rights = [rows(right, u) for u in range(4)]
    out = []
    for side in (left, turned):
        for s in range(4):
            own = rows(side, s)
            out += [jnp.sum(own * other, axis=0) for other in rights]
    return out if sums is None else [x + y for x, y in zip(sums, out)]


def site_sums(sums):
    stacked = jnp.concatenate([jnp.sum(x, axis=0, keepdims=True) for x in sums], axis=0)
    return jnp.sum(stacked, axis=1, keepdims=True)


def keep(left, turned, at, size, real, imag):
    real, imag = real.reshape(-1, LANES), imag.reshape(-1, LANES)
    left[pl.ds(at, size), :] = real
    left[pl.ds(at + size, size), :] = imag
    if turned is not None:
        turned[pl.ds(at, size), :] = -imag
        turned[pl.ds(at + size, size), :] = real


def kernel(
    sizes, scaling, ranks,
    prop, links, src_h, disp_h, mom_h, perm_h, phase_h,
    out,
    near, near_links, far, far_links, left, turned, right,
    src, disp, mom, perm, phase,
    gathered,
    local_sem, s_send, s_recv, a_recv, line_sem, plane_sem, *link_sems,
):
    ndisp, ng, np_, nz = sizes
    nta, ngz, ngy = ranks
    nsteps = (ndisp - 1) // 2
    size = near.shape[2]
    lane_rows = gathered.shape[1]
    ta, gz, gy = lax.axis_index("ta"), lax.axis_index("gz"), lax.axis_index("gy")
    place = (ta * ngz + gz) * ngy + gy

    loads = [
        pltpu.make_async_copy(a, b, local_sem.at[i])
        for i, (a, b) in enumerate(
            [(prop, near), (links, near_links), (src_h, src), (disp_h, disp),
             (mom_h, mom), (perm_h, perm), (phase_h, phase)]
        )
    ]
    for load in loads:
        load.start()

    depth_peers = [functools.partial(lambda d: (ta, lax.rem(gz + d, ngz), gy), d) for d in range(1, ngz)]
    beside_peers = [functools.partial(lambda d: (ta, gz, lax.rem(gy + d, ngy)), d) for d in range(1, ngy)]
    across_peers = [functools.partial(lambda d: (lax.rem(ta + d, nta), gz, gy), d) for d in range(1, nta)]

    def greet(semaphore, peers):
        for at in peers:
            pl.semaphore_signal(semaphore, inc=1, device_id=at(), device_id_type=MESH)

    count = nta * ngz * ngy
    barrier = pltpu.get_barrier_semaphore()
    greet(barrier, depth_peers + beside_peers + across_peers)
    pl.semaphore_wait(barrier, ngz + ngy + nta - 3)

    def target(k):
        return (ta, lax.rem(gz + ngz - k, ngz), gy)

    sends = [
        [
            pltpu.make_async_remote_copy(
                src_ref=near.at[:, c], dst_ref=far.at[k - 1, :, c], send_sem=s_send.at[0],
                recv_sem=s_recv.at[k - 1, c], device_id=target(k), device_id_type=MESH)
            for c in range(3)
        ]
        for k in range(1, nsteps + 1)
    ]
    u_send, u_recv = link_sems if link_sems else (None, None)
    link_sends = [
        pltpu.make_async_remote_copy(
            src_ref=near_links, dst_ref=far_links.at[k - 1], send_sem=u_send.at[k - 1],
            recv_sem=u_recv.at[k - 1], device_id=target(k), device_id_type=MESH)
        for k in range(1, nsteps)
    ]
    loads[0].wait()
    for c in range(3):
        for copies in sends:
            copies[c].start()
    loads[1].wait()
    for copy in link_sends:
        copy.start()
    greet(line_sem.at[0], depth_peers)
    for load in loads[2:]:
        load.wait()

    sums = None
    for c in range(3):
        keep(left, turned, 2 * size * c, size, near[0, c].astype(jnp.float32), near[1, c].astype(jnp.float32))
        sums = add_pairs(sums, left, turned, left, 2 * size * c, 2 * size)
    totals = [site_sums(sums)]
    pl.semaphore_wait(line_sem.at[0], ngz - 1)
    greet(plane_sem.at[0], across_peers)
    tables = [
        weights(h, sizes, (src, disp, mom, perm, phase), (ta, gz), scaling)
        for h in range(lane_rows)
    ]

    def link_at(ref):
        return [
            [
                [jnp.broadcast_to(ref[3 * a + b, pl.ds(part, 1), :].astype(jnp.float32), (8, LANES))
                 for part in range(2)]
                for b in range(3)
            ]
            for a in range(3)
        ]

    wilson = None
    for k in range(1, nsteps + 1):
        if k == 1:
            wilson = link_at(near_links)
        else:
            link_sends[k - 2].wait_recv()
            step = link_at(far_links.at[k - 2])
            wilson = [
                [
                    [
                        sum(wilson[a][c][0] * step[c][b][0] - wilson[a][c][1] * step[c][b][1] for c in range(3)),
                        sum(wilson[a][c][0] * step[c][b][1] + wilson[a][c][1] * step[c][b][0] for c in range(3)),
                    ]
                    for b in range(3)
                ]
                for a in range(3)
            ]
        for chunk in range(size // 16):
            field = [
                [
                    near[part, a, pl.ds(chunk * 16, 16), :].astype(jnp.float32).reshape(2, 8, LANES)
                    for a in range(3)
                ]
                for part in range(2)
            ]
            for b in range(3):
                real = sum(field[0][a] * wilson[a][b][0] + field[1][a] * wilson[a][b][1] for a in range(3))
                imag = sum(field[1][a] * wilson[a][b][0] - field[0][a] * wilson[a][b][1] for a in range(3))
                real, imag = real.reshape(16, LANES), imag.reshape(16, LANES)
                at = 2 * size * b + chunk * 16
                left[pl.ds(at, 16), :] = real
                left[pl.ds(at + size, 16), :] = imag
                turned[pl.ds(at, 16), :] = -imag
                turned[pl.ds(at + size, 16), :] = real
        sums = None
        for c in range(3):
            sends[k - 1][c].wait_recv()
            keep(right, None, 2 * size * c, size,
                 far[k - 1, 0, c].astype(jnp.float32), far[k - 1, 1, c].astype(jnp.float32))
            sums = add_pairs(sums, left, turned, right, 2 * size * c, 2 * size)
        totals.append(site_sums(sums))

    for h in range(lane_rows):
        table, reach = tables[h]
        chosen = jnp.zeros(table.shape, jnp.float32)
        for k in range(nsteps + 1):
            chosen = jnp.where(reach == k, totals[k], chosen)
        gathered[place, pl.ds(h, 1), :] = jnp.sum(chosen * table, axis=0, keepdims=True)

    pl.semaphore_wait(plane_sem.at[0], nta - 1)
    pltpu.make_async_copy(far, far, s_send.at[0]).wait()
    each(
        ranks,
        place,
        lambda at: pltpu.make_async_remote_copy(
            src_ref=gathered.at[place], dst_ref=gathered.at[place], send_sem=s_send.at[0],
            recv_sem=a_recv.at[0], device_id=at, device_id_type=MESH).start(),
    )
    others = gathered.at[pl.ds(0, count - 1)]
    pltpu.make_async_copy(others, others, a_recv.at[0]).wait()
    for t in range(nta):
        block = gathered[pl.ds(t * ngz * ngy, ngz * ngy)]
        out[t] = jnp.sum(block, axis=0)
    for copy in link_sends:
        copy.wait_send()
    pltpu.make_async_copy(others, others, s_send.at[0]).wait()


def each(ranks, place, act):
    nta, ngz, ngy = ranks
    count = nta * ngz * ngy

    def one(step, along):
        beside = step // (nta * ngz)
        across = step // ngz % nta

        @pl.when(place != (across * ngz + along) * ngy + beside)
        def _():
            act((across, along, beside))

    if count > 64:
        lax.fori_loop(0, count, lambda step, carry: (one(step, step % ngz), carry)[1], 0)
        return
    for step in range(count):
        one(step, step % ngz)


def body(ranks, propagator, links, source_z, displacements, momenta, gamma_perm, gamma_phase):
    nta, ngz, ngy = ranks
    sites = propagator.shape[6]
    ndisp, np_, ng = displacements.shape[0], momenta.shape[0], gamma_perm.shape[0]
    nsteps = (ndisp - 1) // 2
    sizes = (ndisp, ng, np_, ngz)
    scaling = 1.0 / (24.0 * math.sqrt(sites * ngy * ngz))
    field = jnp.transpose(propagator, (0, 2, 3, 4, 5, 1, 6)).reshape(2, 3, -1, sites)
    link = jnp.transpose(links, (1, 2, 3, 4, 0, 5)).reshape(9, 2, sites)
    size = field.shape[2]
    regular = pltpu.SemaphoreType.REGULAR
    lane_rows = -(-ndisp * ng * np_ * 2 // LANES)
    more = max(nsteps - 1, 1)
    dma = pltpu.SemaphoreType.DMA
    reduced = pl.pallas_call(
        functools.partial(kernel, sizes, scaling, ranks),
        out_shape=pltpu.VMEM((nta, lane_rows, LANES), jnp.float32),
        in_specs=[pl.BlockSpec(memory_space=pltpu.HBM)] * 7,
        out_specs=pl.BlockSpec(memory_space=pltpu.VMEM),
        scratch_shapes=[
            pltpu.VMEM((2, 3, size, sites), jnp.bfloat16),
            pltpu.VMEM((9, 2, sites), jnp.bfloat16),
            pltpu.VMEM((nsteps, 2, 3, size, sites), jnp.bfloat16),
            pltpu.VMEM((more, 9, 2, sites), jnp.bfloat16),
            pltpu.VMEM((6 * size, sites), jnp.float32),
            pltpu.VMEM((6 * size, sites), jnp.float32),
            pltpu.VMEM((6 * size, sites), jnp.float32),
            pltpu.SMEM(source_z.shape, jnp.int32),
            pltpu.SMEM(displacements.shape, jnp.int32),
            pltpu.SMEM(momenta.shape, jnp.int32),
            pltpu.SMEM(gamma_perm.shape, jnp.int32),
            pltpu.SMEM(gamma_phase.shape, jnp.int32),
            pltpu.VMEM((nta * ngz * ngy, lane_rows, LANES), jnp.float32),
            dma((7,)), dma((1,)), dma((nsteps, 3)),
            dma((1,)), regular((1,)), regular((1,)),
        ] + [dma((nsteps - 1,))] * (2 if nsteps > 1 else 0),
        compiler_params=pltpu.CompilerParams(collective_id=0, has_side_effects=True),
    )(field, link, source_z, displacements, momenta, gamma_perm, gamma_phase)
    used = reduced.reshape(nta, lane_rows * LANES)[:, : ndisp * ng * np_ * 2]
    return jnp.swapaxes(used.reshape(nta, ndisp, ng, 2, np_), 3, 4)


def solution(mesh):
    placed = (
        P(None, None, None, None, "ta", "gz", "gy"),
        P(None, None, None, "ta", "gz", "gy"),
        P(),
        P(),
        P(),
        P(),
        P(),
    )
    ranks = tuple(mesh.shape[axis] for axis in ("ta", "gz", "gy"))
    return jax.shard_map(
        functools.partial(body, ranks), mesh=mesh, in_specs=placed, out_specs=P(), check_vma=False
    )
```

profile of v0, /device:TPU:0, one launch (start us, length us, event | category | flops | bytes accessed | tf_op | source)
XLA Modules:
  0.0 13.0 jit_solution(17325010067072506363)
XLA Ops:
  0.0 12.3 %shard_map.73 = f32[2,1,128]{2,1,0:T(1,128)S(1)} custom-call(bf16[2,3,48,128]{3,2,1,0:T(8,128)(2,1)} %bitcast.10, bf16[9,2,128]{2,1,0:T(2,128)(2,1)} %bitcast.11, s32[2,4]{1,0:T(2,128)} %src_h.1, s32[3]{0:T(128)} %disp_h.1, s32[4]{0:T(128)} %mom_h.1, s32[4,4]{1,0:T(4,128)} %perm_h.1, s32[4,4]{1,0:T(4,128)} %phase_h.1), custom_call_target="tpu_custom_call" | custom-call | tf_op jit(solution)/shard_map/pallas_call | solution.py:281
  12.3 0.7 %reshape.15 = f32[2,3,4,2,4]{4,3,2,1,0:T(2,128)} reshape(f32[2,96]{1,0:T(2,128)S(1)} %bitcast.9) | data formatting | bytes 1536 | tf_op jit(solution)/shard_map/reshape | solution.py:306
where the time goes:
time: 13.2 us; the launch traced here: 13 us
  Pallas kernels  12.3 us (93%)
  local copies, waits for them, and re-layouts  0.72 us (5%)
    pallas_call x1, Pallas kernels, body(): pl.pallas_call(functools.partial(kernel, sizes, scaling, ranks), out_shap...  12.3 us
    reshape x1, local copies, waits for them, and re-layouts, body(): return jnp.swapaxes(used.reshape(nta, ndisp, ng, 2, np_), 3, 4)  0.72 us

commit v1 on v0

--- a/solution.py
+++ b/solution.py
@@ -92,7 +92,7 @@
     near, near_links, far, far_links, left, turned, right,
     src, disp, mom, perm, phase,
     gathered,
-    local_sem, s_send, s_recv, a_recv, line_sem, plane_sem, *link_sems,
+    local_sem, s_send, s_recv, a_send, a_recv, low_sem, line_sem, plane_sem, *link_sems,
 ):
     ndisp, ng, np_, nz = sizes
     nta, ngz, ngy = ranks
@@ -112,18 +112,52 @@
     for load in loads:
         load.start()
 
-    depth_peers = [functools.partial(lambda d: (ta, lax.rem(gz + d, ngz), gy), d) for d in range(1, ngz)]
-    beside_peers = [functools.partial(lambda d: (ta, gz, lax.rem(gy + d, ngy)), d) for d in range(1, ngy)]
-    across_peers = [functools.partial(lambda d: (lax.rem(ta + d, nta), gz, gy), d) for d in range(1, nta)]
-
-    def greet(semaphore, peers):
-        for at in peers:
-            pl.semaphore_signal(semaphore, inc=1, device_id=at(), device_id_type=MESH)
+    lines = [
+        (gz, ngz, lambda i: (ta, i, gy)),
+        (gy, ngy, lambda i: (ta, gz, i)),
+        (ta, nta, lambda i: (i, gz, gy)),
+    ]
+
+    def greet(semaphore, at):
+        pl.semaphore_signal(semaphore, inc=1, device_id=at, device_id_type=MESH)
+
+    def greet_span(semaphore, line, low, high):
+        lax.fori_loop(low, high, lambda i, carry: (greet(semaphore, line[2](i)), carry)[1], 0)
+
+    def greet_line(semaphore, line):
+        greet_span(semaphore, line, 0, line[0])
+        greet_span(semaphore, line, line[0] + 1, line[1])
 
     count = nta * ngz * ngy
     barrier = pltpu.get_barrier_semaphore()
-    greet(barrier, depth_peers + beside_peers + across_peers)
-    pl.semaphore_wait(barrier, ngz + ngy + nta - 3)
+    for k in range(1, nsteps + 1):
+        @pl.when(gz + k >= ngz)
+        def _():
+            greet(barrier, (ta, gz + k - ngz, gy))
+    for line in lines:
+        greet_span(barrier, line, line[0] + 1, line[1])
+    nroots = min(2, ngz)
+    is_root = (ta + gy == 0) & (gz < nroots)
+
+    @pl.when(is_root)
+    def _():
+        def one(step, carry):
+            at = (step // (ngz * ngy), step // ngy % ngz, step % ngy)
+
+            @pl.when(step != place)
+            def _():
+                greet(barrier, at)
+
+            return carry
+
+        lax.fori_loop(0, count, one, 0)
+
+    pl.semaphore_wait(
+        barrier,
+        jnp.maximum(gz, nsteps) + gy + ta + nroots - jnp.where(is_root, 1, 0),
+    )
+    for line in lines:
+        greet_span(low_sem.at[0], line, 0, line[0])
 
     def target(k):
         return (ta, lax.rem(gz + ngz - k, ngz), gy)
@@ -151,7 +185,6 @@
     loads[1].wait()
     for copy in link_sends:
         copy.start()
-    greet(line_sem.at[0], depth_peers)
     for load in loads[2:]:
         load.wait()
 
@@ -160,8 +193,13 @@
         keep(left, turned, 2 * size * c, size, near[0, c].astype(jnp.float32), near[1, c].astype(jnp.float32))
         sums = add_pairs(sums, left, turned, left, 2 * size * c, 2 * size)
     totals = [site_sums(sums)]
-    pl.semaphore_wait(line_sem.at[0], ngz - 1)
-    greet(plane_sem.at[0], across_peers)
+    later = (ngz - 1 - gz) + (ngy - 1 - gy) + (nta - 1 - ta)
+
+    @pl.when(later > 0)
+    def _():
+        pl.semaphore_wait(low_sem.at[0], later)
+
+    greet_line(line_sem.at[0], lines[0])
     tables = [
         weights(h, sizes, (src, disp, mom, perm, phase), (ta, gz), scaling)
         for h in range(lane_rows)
@@ -211,6 +249,9 @@
                 left[pl.ds(at + size, 16), :] = imag
                 turned[pl.ds(at, 16), :] = -imag
                 turned[pl.ds(at + size, 16), :] = real
+        if k == nsteps:
+            pl.semaphore_wait(line_sem.at[0], ngz - 1)
+            greet_line(plane_sem.at[0], lines[2])
         sums = None
         for c in range(3):
             sends[k - 1][c].wait_recv()
@@ -226,15 +267,17 @@
             chosen = jnp.where(reach == k, totals[k], chosen)
         gathered[place, pl.ds(h, 1), :] = jnp.sum(chosen * table, axis=0, keepdims=True)
 
+    def give(at):
+        pltpu.make_async_remote_copy(
+            src_ref=gathered.at[place], dst_ref=gathered.at[place], send_sem=a_send.at[0],
+            recv_sem=a_recv.at[0], device_id=at, device_id_type=MESH).start()
+
+    for root in range(nroots):
+        @pl.when(place != root * ngy)
+        def _():
+            give((0, root, 0))
     pl.semaphore_wait(plane_sem.at[0], nta - 1)
-    pltpu.make_async_copy(far, far, s_send.at[0]).wait()
-    each(
-        ranks,
-        place,
-        lambda at: pltpu.make_async_remote_copy(
-            src_ref=gathered.at[place], dst_ref=gathered.at[place], send_sem=s_send.at[0],
-            recv_sem=a_recv.at[0], device_id=at, device_id_type=MESH).start(),
-    )
+    each(ranks, place, nroots, give)
     others = gathered.at[pl.ds(0, count - 1)]
     pltpu.make_async_copy(others, others, a_recv.at[0]).wait()
     for t in range(nta):
@@ -242,10 +285,11 @@
         out[t] = jnp.sum(block, axis=0)
     for copy in link_sends:
         copy.wait_send()
-    pltpu.make_async_copy(others, others, s_send.at[0]).wait()
-
-
-def each(ranks, place, act):
+    pltpu.make_async_copy(far, far, s_send.at[0]).wait()
+    pltpu.make_async_copy(others, others, a_send.at[0]).wait()
+
+
+def each(ranks, place, start, act):
     nta, ngz, ngy = ranks
     count = nta * ngz * ngy
 
@@ -258,9 +302,9 @@
             act((across, along, beside))
 
     if count > 64:
-        lax.fori_loop(0, count, lambda step, carry: (one(step, step % ngz), carry)[1], 0)
+        lax.fori_loop(start, count, lambda step, carry: (one(step, step % ngz), carry)[1], 0)
         return
-    for step in range(count):
+    for step in range(start, count):
         one(step, step % ngz)
 
 
@@ -298,7 +342,7 @@
             pltpu.SMEM(gamma_phase.shape, jnp.int32),
             pltpu.VMEM((nta * ngz * ngy, lane_rows, LANES), jnp.float32),
             dma((7,)), dma((1,)), dma((nsteps, 3)),
-            dma((1,)), regular((1,)), regular((1,)),
+            dma((1,)), dma((1,)), regular((1,)), regular((1,)), regular((1,)),
         ] + [dma((nsteps - 1,))] * (2 if nsteps > 1 else 0),
         compiler_params=pltpu.CompilerParams(collective_id=0, has_side_effects=True),
     )(field, link, source_z, displacements, momenta, gamma_perm, gamma_phase)

time: 13.2 us -> 12.6 us (0.955)
  Pallas kernels: 12.3 us -> 11.8 us
    pallas_call x1, Pallas kernels: 12.3 us -> 11.8 us  [body(): pl.pallas_call(functools.partial(kernel, sizes, scaling, ranks), out_shap...]
where the time goes in v1:
time: 12.6 us; the launch traced here: 12.5 us
  Pallas kernels  11.8 us (94%)
  local copies, waits for them, and re-layouts  0.72 us (6%)
    pallas_call x1, Pallas kernels, body(): pl.pallas_call(functools.partial(kernel, sizes, scaling, ranks), out_shap...  11.8 us
    reshape x1, local copies, waits for them, and re-layouts, body(): return jnp.swapaxes(used.reshape(nta, ndisp, ng, 2, np_), 3, 4)  0.72 us

profile of v1, /device:TPU:0, one launch (start us, length us, event | category | flops | bytes accessed | tf_op | source)
XLA Modules:
  0.0 12.5 jit_solution(1821315158016722694)
XLA Ops:
  0.0 11.8 %shard_map.73 = f32[2,1,128]{2,1,0:T(1,128)S(1)} custom-call(bf16[2,3,48,128]{3,2,1,0:T(8,128)(2,1)} %bitcast.10, bf16[9,2,128]{2,1,0:T(2,128)(2,1)} %bitcast.11, s32[2,4]{1,0:T(2,128)} %src_h.1, s32[3]{0:T(128)} %disp_h.1, s32[4]{0:T(128)} %mom_h.1, s32[4,4]{1,0:T(4,128)} %perm_h.1, s32[4,4]{1,0:T(4,128)} %phase_h.1), custom_call_target="tpu_custom_call" | custom-call | tf_op jit(solution)/shard_map/pallas_call | solution.py:325
  11.8 0.7 %reshape.15 = f32[2,3,4,2,4]{4,3,2,1,0:T(2,128)} reshape(f32[2,96]{1,0:T(2,128)S(1)} %bitcast.9) | data formatting | bytes 1536 | tf_op jit(solution)/shard_map/reshape | solution.py:350

commit v2 on v1

--- a/solution.py
+++ b/solution.py
@@ -18,9 +18,10 @@
     slice_at, depth_at = place
     nsteps = (ndisp - 1) // 2
     shape = (32, LANES)
-    lane = lax.broadcasted_iota(jnp.int32, shape, 1) + lane_row * LANES
+    lane = lax.broadcasted_iota(jnp.int32, shape, 1)
+    momentum = lane & (np_ - 1)
+    lane = lane_row * LANES + LANES - np_ - (lane - momentum)
     row = lax.broadcasted_iota(jnp.int32, shape, 0)
-    momentum = lane & (np_ - 1)
     out_part = (lane // np_) & 1
     gamma = (lane // (2 * np_)) & (ng - 1)
     entry = lane // (2 * np_ * ng)
@@ -92,7 +93,7 @@
     near, near_links, far, far_links, left, turned, right,
     src, disp, mom, perm, phase,
     gathered,
-    local_sem, s_send, s_recv, a_send, a_recv, low_sem, line_sem, plane_sem, *link_sems,
+    local_sem, s_send, s_recv, a_recv, low_sem, line_sem, plane_sem, *link_sems,
 ):
     ndisp, ng, np_, nz = sizes
     nta, ngz, ngy = ranks
@@ -105,12 +106,15 @@
     loads = [
         pltpu.make_async_copy(a, b, local_sem.at[i])
         for i, (a, b) in enumerate(
-            [(prop, near), (links, near_links), (src_h, src), (disp_h, disp),
-             (mom_h, mom), (perm_h, perm), (phase_h, phase)]
+            [(prop.at[:, c], near.at[:, c]) for c in range(3)] + [(links, near_links)]
         )
     ]
-    for load in loads:
-        load.start()
+    smalls = [
+        pltpu.make_async_copy(a, b, local_sem.at[i])
+        for i, (a, b) in enumerate(
+            [(src_h, src), (disp_h, disp), (mom_h, mom), (perm_h, perm), (phase_h, phase)]
+        )
+    ]
 
     lines = [
         (gz, ngz, lambda i: (ta, i, gy)),
@@ -134,6 +138,8 @@
         @pl.when(gz + k >= ngz)
         def _():
             greet(barrier, (ta, gz + k - ngz, gy))
+    for load in loads:
+        load.start()
     for line in lines:
         greet_span(barrier, line, line[0] + 1, line[1])
     nroots = min(2, ngz)
@@ -156,8 +162,6 @@
         barrier,
         jnp.maximum(gz, nsteps) + gy + ta + nroots - jnp.where(is_root, 1, 0),
     )
-    for line in lines:
-        greet_span(low_sem.at[0], line, 0, line[0])
 
     def target(k):
         return (ta, lax.rem(gz + ngz - k, ngz), gy)
@@ -178,28 +182,39 @@
             recv_sem=u_recv.at[k - 1], device_id=target(k), device_id_type=MESH)
         for k in range(1, nsteps)
     ]
-    loads[0].wait()
     for c in range(3):
+        loads[c].wait()
         for copies in sends:
             copies[c].start()
-    loads[1].wait()
+    for line in lines:
+        greet_span(low_sem.at[0], line, 0, line[0])
+    loads[3].wait()
+    for small in smalls:
+        small.start()
     for copy in link_sends:
         copy.start()
-    for load in loads[2:]:
-        load.wait()
-
     sums = None
     for c in range(3):
         keep(left, turned, 2 * size * c, size, near[0, c].astype(jnp.float32), near[1, c].astype(jnp.float32))
         sums = add_pairs(sums, left, turned, left, 2 * size * c, 2 * size)
     totals = [site_sums(sums)]
+    for small in smalls:
+        small.wait()
     later = (ngz - 1 - gz) + (ngy - 1 - gy) + (nta - 1 - ta)
-
-    @pl.when(later > 0)
-    def _():
-        pl.semaphore_wait(low_sem.at[0], later)
-
-    greet_line(line_sem.at[0], lines[0])
+    inner = lax.rem(gz, 2) == 0
+
+    def meet_depth():
+        @pl.when(later > 0)
+        def _():
+            pl.semaphore_wait(low_sem.at[0], later)
+
+        greet_line(line_sem.at[0], lines[0])
+
+    def meet_across():
+        pl.semaphore_wait(line_sem.at[0], ngz - 1)
+        greet_line(plane_sem.at[0], lines[2])
+
+    pl.when(jnp.logical_not(inner))(meet_depth)
     tables = [
         weights(h, sizes, (src, disp, mom, perm, phase), (ta, gz), scaling)
         for h in range(lane_rows)
@@ -249,11 +264,10 @@
                 left[pl.ds(at + size, 16), :] = imag
                 turned[pl.ds(at, 16), :] = -imag
                 turned[pl.ds(at + size, 16), :] = real
-        if k == nsteps:
-            pl.semaphore_wait(line_sem.at[0], ngz - 1)
-            greet_line(plane_sem.at[0], lines[2])
         sums = None
         for c in range(3):
+            if k == nsteps and c == 2:
+                pl.when(jnp.logical_not(inner))(meet_across)
             sends[k - 1][c].wait_recv()
             keep(right, None, 2 * size * c, size,
                  far[k - 1, 0, c].astype(jnp.float32), far[k - 1, 1, c].astype(jnp.float32))
@@ -269,24 +283,43 @@
 
     def give(at):
         pltpu.make_async_remote_copy(
-            src_ref=gathered.at[place], dst_ref=gathered.at[place], send_sem=a_send.at[0],
+            src_ref=gathered.at[place], dst_ref=gathered.at[place], send_sem=s_send.at[0],
             recv_sem=a_recv.at[0], device_id=at, device_id_type=MESH).start()
 
     for root in range(nroots):
         @pl.when(place != root * ngy)
         def _():
             give((0, root, 0))
+    @pl.when(inner)
+    def _():
+        meet_depth()
+        meet_across()
+
     pl.semaphore_wait(plane_sem.at[0], nta - 1)
     each(ranks, place, nroots, give)
     others = gathered.at[pl.ds(0, count - 1)]
     pltpu.make_async_copy(others, others, a_recv.at[0]).wait()
     for t in range(nta):
-        block = gathered[pl.ds(t * ngz * ngy, ngz * ngy)]
-        out[t] = jnp.sum(block, axis=0)
+        for h in range(lane_rows):
+            total = row_sum(gathered, t * ngz * ngy, ngz * ngy, h)
+            low = h * (LANES // np_)
+            for row in range(low, min(low + LANES // np_, out.shape[1]), 8):
+                shift = (1 + row - low) * np_
+                out[t, pl.ds(row, 8), :] = pltpu.roll(total, shift, 1, stride=np_, stride_axis=0)[:, :np_]
     for copy in link_sends:
         copy.wait_send()
     pltpu.make_async_copy(far, far, s_send.at[0]).wait()
-    pltpu.make_async_copy(others, others, a_send.at[0]).wait()
+    pltpu.make_async_copy(others, others, s_send.at[0]).wait()
+
+
+def row_sum(ref, start, size, h):
+    if size > 32:
+        total = jnp.sum(ref[pl.ds(start, size), pl.ds(h, 1), :], axis=0)
+        return jnp.broadcast_to(total, (8, LANES))
+    terms = [jnp.broadcast_to(ref[start + i, pl.ds(h, 1), :], (8, LANES)) for i in range(size)]
+    while len(terms) > 1:
+        terms = [sum(terms[i:i + 2]) for i in range(0, len(terms), 2)]
+    return terms[0]
 
 
 def each(ranks, place, start, act):
@@ -324,7 +357,7 @@
     dma = pltpu.SemaphoreType.DMA
     reduced = pl.pallas_call(
         functools.partial(kernel, sizes, scaling, ranks),
-        out_shape=pltpu.VMEM((nta, lane_rows, LANES), jnp.float32),
+        out_shape=pltpu.VMEM((nta, ndisp * ng * 2, np_), jnp.float32),
         in_specs=[pl.BlockSpec(memory_space=pltpu.HBM)] * 7,
         out_specs=pl.BlockSpec(memory_space=pltpu.VMEM),
         scratch_shapes=[
@@ -341,13 +374,12 @@
             pltpu.SMEM(gamma_perm.shape, jnp.int32),
             pltpu.SMEM(gamma_phase.shape, jnp.int32),
             pltpu.VMEM((nta * ngz * ngy, lane_rows, LANES), jnp.float32),
-            dma((7,)), dma((1,)), dma((nsteps, 3)),
-            dma((1,)), dma((1,)), regular((1,)), regular((1,)), regular((1,)),
+            dma((5,)), dma((1,)), dma((nsteps, 3)),
+            dma((1,)), regular((1,)), regular((1,)), regular((1,)),
         ] + [dma((nsteps - 1,))] * (2 if nsteps > 1 else 0),
         compiler_params=pltpu.CompilerParams(collective_id=0, has_side_effects=True),
     )(field, link, source_z, displacements, momenta, gamma_perm, gamma_phase)
-    used = reduced.reshape(nta, lane_rows * LANES)[:, : ndisp * ng * np_ * 2]
-    return jnp.swapaxes(used.reshape(nta, ndisp, ng, 2, np_), 3, 4)
+    return jnp.swapaxes(reduced.reshape(nta, ndisp, ng, 2, np_), 3, 4)
 
 
 def solution(mesh):

time: 12.6 us -> 12.6 us (level)
    reshape x1 -> x0, local copies, waits for them, and re-layouts: 0.72 us -> none  [body(): return jnp.swapaxes(used.reshape(nta, ndisp, ng, 2, np_), 3, 4)]
    unnamed x0 -> x1, local copies, waits for them, and re-layouts: none -> 0.61 us
where the time goes in v2:
time: 12.6 us; the launch traced here: 12.4 us
  Pallas kernels  11.8 us (94%)
  local copies, waits for them, and re-layouts  0.61 us (5%)
    pallas_call x1, Pallas kernels, body(): pl.pallas_call(functools.partial(kernel, sizes, scaling, ranks), out_shap...  11.8 us
    unnamed x1, local copies, waits for them, and re-layouts  0.61 us

profile of v2, /device:TPU:0, one launch (start us, length us, event | category | flops | bytes accessed | tf_op | source)
XLA Modules:
  0.0 12.4 jit_solution(9917433316923217441)
XLA Ops:
  0.0 11.8 %shard_map.73 = f32[2,24,4]{2,1,0:T(8,128)S(1)} custom-call(bf16[2,3,48,128]{3,2,1,0:T(8,128)(2,1)} %bitcast.10, bf16[9,2,128]{2,1,0:T(2,128)(2,1)} %bitcast.11, s32[2,4]{1,0:T(2,128)} %src_h.1, s32[3]{0:T(128)} %disp_h.1, s32[4]{0:T(128)} %mom_h.1, s32[4,4]{1,0:T(4,128)} %perm_h.1, s32[4,4]{1,0:T(4,128)} %phase_h.1), custom_call_target="tpu_custom_call" | custom-call | tf_op jit(solution)/shard_map/pallas_call | solution.py:358
  11.8 0.6 %copy.9 = f32[2,3,4,4,2]{3,4,2,1,0:T(2,128)} copy(f32[2,3,4,4,2]{3,4,2,1,0:T(2,128)S(1)} %bitcast.9) | data formatting | bytes 1536

commit v3 on v2

--- a/solution.py
+++ b/solution.py
@@ -86,15 +86,78 @@
         turned[pl.ds(at + size, size), :] = real
 
 
-def kernel(
-    sizes, scaling, ranks,
-    prop, links, src_h, disp_h, mom_h, perm_h, phase_h,
-    out,
-    near, near_links, far, far_links, left, turned, right,
-    src, disp, mom, perm, phase,
-    gathered,
-    local_sem, s_send, s_recv, a_recv, low_sem, line_sem, plane_sem, *link_sems,
-):
+def self_sums(field, left, turned, size):
+    sums = None
+    for c in range(3):
+        keep(left, turned, 2 * size * c, size, field[0, c].astype(jnp.float32), field[1, c].astype(jnp.float32))
+        sums = add_pairs(sums, left, turned, left, 2 * size * c, 2 * size)
+    return site_sums(sums)
+
+
+def link_at(ref):
+    return [
+        [
+            [jnp.broadcast_to(ref[3 * a + b, pl.ds(part, 1), :].astype(jnp.float32), (8, LANES))
+             for part in range(2)]
+            for b in range(3)
+        ]
+        for a in range(3)
+    ]
+
+
+def carry_link(near, wilson, left, turned, size):
+    for chunk in range(size // 16):
+        field = [
+            [
+                near[part, a, pl.ds(chunk * 16, 16), :].astype(jnp.float32).reshape(2, 8, LANES)
+                for a in range(3)
+            ]
+            for part in range(2)
+        ]
+        for b in range(3):
+            real = sum(field[0][a] * wilson[a][b][0] + field[1][a] * wilson[a][b][1] for a in range(3))
+            imag = sum(field[1][a] * wilson[a][b][0] - field[0][a] * wilson[a][b][1] for a in range(3))
+            real, imag = real.reshape(16, LANES), imag.reshape(16, LANES)
+            at = 2 * size * b + chunk * 16
+            left[pl.ds(at, 16), :] = real
+            left[pl.ds(at + size, 16), :] = imag
+            turned[pl.ds(at, 16), :] = -imag
+            turned[pl.ds(at + size, 16), :] = real
+
+
+def pair_sums(far, left, turned, right, size, before):
+    sums = None
+    for c in range(3):
+        before(c)
+        keep(right, None, 2 * size * c, size, far[0, c].astype(jnp.float32), far[1, c].astype(jnp.float32))
+        sums = add_pairs(sums, left, turned, right, 2 * size * c, 2 * size)
+    return site_sums(sums)
+
+
+def row_of(totals, table, reach):
+    chosen = jnp.zeros(table.shape, jnp.float32)
+    for k, total in enumerate(totals):
+        chosen = jnp.where(reach == k, total, chosen)
+    return jnp.sum(chosen * table, axis=0, keepdims=True)
+
+
+def kernel(sizes, scaling, ranks, helped, *refs):
+    refs = list(refs)
+    prop, links, src_h, disp_h, mom_h, perm_h, phase_h, out = refs[:8]
+    near, near_links, far, far_links, left, turned, right = refs[8:15]
+    rest = refs[15:]
+    heap = heap_links = heap_left = heap_turned = heap_tables = None
+    if helped:
+        heap, heap_links, heap_left, heap_turned, heap_tables = rest[:5]
+        rest = rest[5:]
+    src, disp, mom, perm, phase, gathered = rest[:6]
+    local_sem, s_send, s_recv, a_recv, low_sem, line_sem, plane_sem = rest[6:13]
+    rest = rest[13:]
+    heap_recv = heap_links_recv = None
+    if helped:
+        heap_recv, heap_links_recv = rest[:2]
+        rest = rest[2:]
+    link_sems = rest
     ndisp, ng, np_, nz = sizes
     nta, ngz, ngy = ranks
     nsteps = (ndisp - 1) // 2
@@ -144,6 +207,14 @@
         greet_span(barrier, line, line[0] + 1, line[1])
     nroots = min(2, ngz)
     is_root = (ta + gy == 0) & (gz < nroots)
+    helper_at = (0, nroots - 1, 0)
+    is_helper = (ta + gy == 0) & (gz == nroots - 1)
+    is_distant = (ta == nta - 1) & (gy == ngy - 1)
+    is_served = is_distant & (lax.rem(gz, 2) == 1)
+    served = list(range(1, ngz, 2)) if helped else []
+
+    def place_of(z):
+        return ((nta - 1) * ngz + z) * ngy + ngy - 1
 
     @pl.when(is_root)
     def _():
@@ -189,15 +260,23 @@
     for line in lines:
         greet_span(low_sem.at[0], line, 0, line[0])
     loads[3].wait()
+    if helped:
+        @pl.when(is_distant)
+        def _():
+            pltpu.make_async_remote_copy(
+                src_ref=near, dst_ref=heap.at[gz], send_sem=s_send.at[0], recv_sem=heap_recv.at[gz],
+                device_id=helper_at, device_id_type=MESH).start()
+
+        @pl.when(is_served)
+        def _():
+            pltpu.make_async_remote_copy(
+                src_ref=near_links, dst_ref=heap_links.at[gz // 2], send_sem=s_send.at[0],
+                recv_sem=heap_links_recv.at[gz // 2], device_id=helper_at, device_id_type=MESH).start()
     for small in smalls:
         small.start()
     for copy in link_sends:
         copy.start()
-    sums = None
-    for c in range(3):
-        keep(left, turned, 2 * size * c, size, near[0, c].astype(jnp.float32), near[1, c].astype(jnp.float32))
-        sums = add_pairs(sums, left, turned, left, 2 * size * c, 2 * size)
-    totals = [site_sums(sums)]
+    totals = [self_sums(near, left, turned, size)]
     for small in smalls:
         small.wait()
     later = (ngz - 1 - gz) + (ngy - 1 - gy) + (nta - 1 - ta)
@@ -220,15 +299,13 @@
         for h in range(lane_rows)
     ]
 
-    def link_at(ref):
-        return [
-            [
-                [jnp.broadcast_to(ref[3 * a + b, pl.ds(part, 1), :].astype(jnp.float32), (8, LANES))
-                 for part in range(2)]
-                for b in range(3)
-            ]
-            for a in range(3)
-        ]
+    if helped:
+        @pl.when(is_helper)
+        def _():
+            for z in served:
+                for h in range(lane_rows):
+                    heap_tables[z // 2, h] = weights(
+                        h, sizes, (src, disp, mom, perm, phase), (nta - 1, z), scaling)[0]
 
     wilson = None
     for k in range(1, nsteps + 1):
@@ -247,47 +324,25 @@
                 ]
                 for a in range(3)
             ]
-        for chunk in range(size // 16):
-            field = [
-                [
-                    near[part, a, pl.ds(chunk * 16, 16), :].astype(jnp.float32).reshape(2, 8, LANES)
-                    for a in range(3)
-                ]
-                for part in range(2)
-            ]
-            for b in range(3):
-                real = sum(field[0][a] * wilson[a][b][0] + field[1][a] * wilson[a][b][1] for a in range(3))
-                imag = sum(field[1][a] * wilson[a][b][0] - field[0][a] * wilson[a][b][1] for a in range(3))
-                real, imag = real.reshape(16, LANES), imag.reshape(16, LANES)
-                at = 2 * size * b + chunk * 16
-                left[pl.ds(at, 16), :] = real
-                left[pl.ds(at + size, 16), :] = imag
-                turned[pl.ds(at, 16), :] = -imag
-                turned[pl.ds(at + size, 16), :] = real
-        sums = None
-        for c in range(3):
+        carry_link(near, wilson, left, turned, size)
+
+        def before(c):
             if k == nsteps and c == 2:
                 pl.when(jnp.logical_not(inner))(meet_across)
             sends[k - 1][c].wait_recv()
-            keep(right, None, 2 * size * c, size,
-                 far[k - 1, 0, c].astype(jnp.float32), far[k - 1, 1, c].astype(jnp.float32))
-            sums = add_pairs(sums, left, turned, right, 2 * size * c, 2 * size)
-        totals.append(site_sums(sums))
+
+        totals.append(pair_sums(far.at[k - 1], left, turned, right, size, before))
 
     for h in range(lane_rows):
-        table, reach = tables[h]
-        chosen = jnp.zeros(table.shape, jnp.float32)
-        for k in range(nsteps + 1):
-            chosen = jnp.where(reach == k, totals[k], chosen)
-        gathered[place, pl.ds(h, 1), :] = jnp.sum(chosen * table, axis=0, keepdims=True)
-
-    def give(at):
+        gathered[place, pl.ds(h, 1), :] = row_of(totals, *tables[h])
+
+    def give(at, row=place):
         pltpu.make_async_remote_copy(
-            src_ref=gathered.at[place], dst_ref=gathered.at[place], send_sem=s_send.at[0],
+            src_ref=gathered.at[row], dst_ref=gathered.at[row], send_sem=s_send.at[0],
             recv_sem=a_recv.at[0], device_id=at, device_id_type=MESH).start()
 
     for root in range(nroots):
-        @pl.when(place != root * ngy)
+        @pl.when((place != root * ngy) & jnp.logical_not(is_served & helped))
         def _():
             give((0, root, 0))
     @pl.when(inner)
@@ -297,8 +352,37 @@
 
     pl.semaphore_wait(plane_sem.at[0], nta - 1)
     each(ranks, place, nroots, give)
-    others = gathered.at[pl.ds(0, count - 1)]
-    pltpu.make_async_copy(others, others, a_recv.at[0]).wait()
+    if helped:
+        @pl.when(is_helper)
+        def _():
+            first = []
+            for z in served:
+                slot = z // 2
+                pltpu.make_async_copy(heap.at[z], heap.at[z], heap_recv.at[z]).wait()
+                pltpu.make_async_copy(heap_links.at[slot], heap_links.at[slot], heap_links_recv.at[slot]).wait()
+                first.append(self_sums(heap.at[z], heap_left.at[slot], heap_turned.at[slot], size))
+                carry_link(heap.at[z], link_at(heap_links.at[slot]), heap_left.at[slot], heap_turned.at[slot], size)
+            for z in reversed(served):
+                slot, other = z // 2, (z + 1) % ngz
+                pltpu.make_async_copy(heap.at[other], heap.at[other], heap_recv.at[other]).wait()
+                pair = pair_sums(
+                    heap.at[other], heap_left.at[slot], heap_turned.at[slot], right, size, lambda c: None)
+                for h in range(lane_rows):
+                    gathered[place_of(z), pl.ds(h, 1), :] = row_of(
+                        [first[slot], pair], heap_tables[slot, h], tables[h][1])
+                for root in range(nroots - 1):
+                    give((0, root, 0), place_of(z))
+
+    def rows_done(semaphore, rows):
+        if rows > 0:
+            pltpu.make_async_copy(gathered.at[pl.ds(0, rows)], gathered.at[pl.ds(0, rows)], semaphore).wait()
+
+    mine = len(served)
+    if helped:
+        pl.when(is_helper)(lambda: rows_done(a_recv.at[0], count - 1 - mine))
+        pl.when(jnp.logical_not(is_helper))(lambda: rows_done(a_recv.at[0], count - 1))
+    else:
+        rows_done(a_recv.at[0], count - 1)
     for t in range(nta):
         for h in range(lane_rows):
             total = row_sum(gathered, t * ngz * ngy, ngz * ngy, h)
@@ -309,7 +393,20 @@
     for copy in link_sends:
         copy.wait_send()
     pltpu.make_async_copy(far, far, s_send.at[0]).wait()
-    pltpu.make_async_copy(others, others, s_send.at[0]).wait()
+    if helped:
+        @pl.when(is_distant)
+        def _():
+            pltpu.make_async_copy(near, near, s_send.at[0]).wait()
+
+        @pl.when(is_served)
+        def _():
+            pltpu.make_async_copy(near_links, near_links, s_send.at[0]).wait()
+
+        pl.when(is_helper)(lambda: rows_done(s_send.at[0], mine * (nroots - 1)))
+        pl.when(jnp.logical_not(is_served))(lambda: rows_done(s_send.at[0], nroots))
+        rows_done(s_send.at[0], count - 1 - nroots)
+    else:
+        rows_done(s_send.at[0], count - 1)
 
 
 def row_sum(ref, start, size, h):
@@ -355,8 +452,18 @@
     lane_rows = -(-ndisp * ng * np_ * 2 // LANES)
     more = max(nsteps - 1, 1)
     dma = pltpu.SemaphoreType.DMA
+    helped = nsteps == 1 and ngz == 4 and nta * ngy > 1
+    pairs = ngz // 2
+    heaps = [
+        pltpu.VMEM((ngz, 2, 3, size, sites), jnp.bfloat16),
+        pltpu.VMEM((pairs, 9, 2, sites), jnp.bfloat16),
+        pltpu.VMEM((pairs, 6 * size, sites), jnp.float32),
+        pltpu.VMEM((pairs, 6 * size, sites), jnp.float32),
+        pltpu.VMEM((pairs, lane_rows, 32, LANES), jnp.float32),
+    ] if helped else []
+    heap_sems = [dma((ngz,)), dma((pairs,))] if helped else []
     reduced = pl.pallas_call(
-        functools.partial(kernel, sizes, scaling, ranks),
+        functools.partial(kernel, sizes, scaling, ranks, helped),
         out_shape=pltpu.VMEM((nta, ndisp * ng * 2, np_), jnp.float32),
         in_specs=[pl.BlockSpec(memory_space=pltpu.HBM)] * 7,
         out_specs=pl.BlockSpec(memory_space=pltpu.VMEM),
@@ -368,6 +475,7 @@
             pltpu.VMEM((6 * size, sites), jnp.float32),
             pltpu.VMEM((6 * size, sites), jnp.float32),
             pltpu.VMEM((6 * size, sites), jnp.float32),
+            *heaps,
             pltpu.SMEM(source_z.shape, jnp.int32),
             pltpu.SMEM(displacements.shape, jnp.int32),
             pltpu.SMEM(momenta.shape, jnp.int32),
@@ -376,6 +484,7 @@
             pltpu.VMEM((nta * ngz * ngy, lane_rows, LANES), jnp.float32),
             dma((5,)), dma((1,)), dma((nsteps, 3)),
             dma((1,)), regular((1,)), regular((1,)), regular((1,)),
+            *heap_sems,
         ] + [dma((nsteps - 1,))] * (2 if nsteps > 1 else 0),
         compiler_params=pltpu.CompilerParams(collective_id=0, has_side_effects=True),
     )(field, link, source_z, displacements, momenta, gamma_perm, gamma_phase)

time: 12.6 us -> 11.8 us (0.937)
  Pallas kernels: 11.8 us -> 11.1 us
    pallas_call x1, Pallas kernels: 11.8 us -> 11.1 us  [body(): pl.pallas_call(functools.partial(kernel, sizes, scaling, ranks, helped),...]
where the time goes in v3:
time: 11.8 us; the launch traced here: 11.7 us
  Pallas kernels  11.1 us (94%)
  local copies, waits for them, and re-layouts  0.61 us (5%)
    pallas_call x1, Pallas kernels, body(): pl.pallas_call(functools.partial(kernel, sizes, scaling, ranks, helped),...  11.1 us
    unnamed x1, local copies, waits for them, and re-layouts  0.61 us

profile of v3, /device:TPU:0, one launch (start us, length us, event | category | flops | bytes accessed | tf_op | source)
XLA Modules:
  0.0 11.7 jit_solution(11870652011074488900)
XLA Ops:
  0.0 11.1 %shard_map.73 = f32[2,24,4]{2,1,0:T(8,128)S(1)} custom-call(bf16[2,3,48,128]{3,2,1,0:T(8,128)(2,1)} %bitcast.10, bf16[9,2,128]{2,1,0:T(2,128)(2,1)} %bitcast.11, s32[2,4]{1,0:T(2,128)} %refs_2_.1, s32[3]{0:T(128)} %refs_3_.1, s32[4]{0:T(128)} %refs_4_.1, s32[4,4]{1,0:T(4,128)} %refs_5_.1, s32[4,4]{1,0:T(4,128)} %refs_6_.1), custom_call_target="tpu_custom_call" | custom-call | tf_op jit(solution)/shard_map/pallas_call | solution.py:465
  11.1 0.6 %copy.9 = f32[2,3,4,4,2]{3,4,2,1,0:T(2,128)} copy(f32[2,3,4,4,2]{3,4,2,1,0:T(2,128)S(1)} %bitcast.9) | data formatting | bytes 1536

commit v4 on v3

--- a/solution.py
+++ b/solution.py
@@ -9,6 +9,7 @@
 from jax.sharding import PartitionSpec as P
 
 MESH = pl.DeviceIdType.MESH
+PIECES = ((0, 2), (2, 1))
 LANES = 128
 
 
@@ -153,10 +154,9 @@
     src, disp, mom, perm, phase, gathered = rest[:6]
     local_sem, s_send, s_recv, a_recv, low_sem, line_sem, plane_sem = rest[6:13]
     rest = rest[13:]
-    heap_recv = heap_links_recv = None
-    if helped:
-        heap_recv, heap_links_recv = rest[:2]
-        rest = rest[2:]
+    heap_recv = None
+    if helped:
+        heap_recv, rest = rest[0], rest[1:]
     link_sems = rest
     ndisp, ng, np_, nz = sizes
     nta, ngz, ngy = ranks
@@ -167,16 +167,14 @@
     place = (ta * ngz + gz) * ngy + gy
 
     loads = [
-        pltpu.make_async_copy(a, b, local_sem.at[i])
+        pltpu.make_async_copy(a, b, local_sem.at[min(i, 2)])
         for i, (a, b) in enumerate(
             [(prop.at[:, c], near.at[:, c]) for c in range(3)] + [(links, near_links)]
         )
     ]
     smalls = [
-        pltpu.make_async_copy(a, b, local_sem.at[i])
-        for i, (a, b) in enumerate(
-            [(src_h, src), (disp_h, disp), (mom_h, mom), (perm_h, perm), (phase_h, phase)]
-        )
+        pltpu.make_async_copy(a, b, local_sem.at[0])
+        for a, b in [(src_h, src), (disp_h, disp), (mom_h, mom), (perm_h, perm), (phase_h, phase)]
     ]
 
     lines = [
@@ -210,7 +208,8 @@
     helper_at = (0, nroots - 1, 0)
     is_helper = (ta + gy == 0) & (gz == nroots - 1)
     is_distant = (ta == nta - 1) & (gy == ngy - 1)
-    is_served = is_distant & (lax.rem(gz, 2) == 1)
+    inner = lax.rem(gz, 2) == 0
+    is_served = is_distant & jnp.logical_not(inner)
     served = list(range(1, ngz, 2)) if helped else []
 
     def place_of(z):
@@ -241,7 +240,7 @@
         [
             pltpu.make_async_remote_copy(
                 src_ref=near.at[:, c], dst_ref=far.at[k - 1, :, c], send_sem=s_send.at[0],
-                recv_sem=s_recv.at[k - 1, c], device_id=target(k), device_id_type=MESH)
+                recv_sem=s_recv.at[k - 1, c // 2], device_id=target(k), device_id_type=MESH)
             for c in range(3)
         ]
         for k in range(1, nsteps + 1)
@@ -255,23 +254,35 @@
     ]
     for c in range(3):
         loads[c].wait()
+        if c == 2:
+            loads[3].wait()
         for copies in sends:
             copies[c].start()
+    if helped:
+        def to_helper(source, slot, semaphore):
+            pltpu.make_async_remote_copy(
+                src_ref=source, dst_ref=slot, send_sem=s_send.at[0], recv_sem=semaphore,
+                device_id=helper_at, device_id_type=MESH).start()
+
+        @pl.when(is_served)
+        def _():
+            to_helper(near, heap.at[gz], heap_recv.at[gz // 2])
+
+        @pl.when(is_distant & (gz == served[0] + 1))
+        def _():
+            for i, piece in enumerate(PIECES):
+                to_helper(near.at[:, pl.ds(*piece)], heap.at[gz, :, pl.ds(*piece)], heap_recv.at[len(served) + i])
+
+        @pl.when(is_distant & inner & (gz != served[0] + 1))
+        def _():
+            slot = lax.rem(gz + ngz - 1, ngz) // 2
+            to_helper(near, heap.at[gz], heap_recv.at[len(PIECES) + len(served) + slot - 1])
     for line in lines:
         greet_span(low_sem.at[0], line, 0, line[0])
-    loads[3].wait()
-    if helped:
-        @pl.when(is_distant)
-        def _():
-            pltpu.make_async_remote_copy(
-                src_ref=near, dst_ref=heap.at[gz], send_sem=s_send.at[0], recv_sem=heap_recv.at[gz],
-                device_id=helper_at, device_id_type=MESH).start()
-
+    if helped:
         @pl.when(is_served)
         def _():
-            pltpu.make_async_remote_copy(
-                src_ref=near_links, dst_ref=heap_links.at[gz // 2], send_sem=s_send.at[0],
-                recv_sem=heap_links_recv.at[gz // 2], device_id=helper_at, device_id_type=MESH).start()
+            to_helper(near_links, heap_links.at[gz // 2], heap_recv.at[gz // 2])
     for small in smalls:
         small.start()
     for copy in link_sends:
@@ -280,7 +291,8 @@
     for small in smalls:
         small.wait()
     later = (ngz - 1 - gz) + (ngy - 1 - gy) + (nta - 1 - ta)
-    inner = lax.rem(gz, 2) == 0
+    outer = jnp.logical_not(inner)
+    early = outer | (gy == ngy - 1)
 
     def meet_depth():
         @pl.when(later > 0)
@@ -293,7 +305,7 @@
         pl.semaphore_wait(line_sem.at[0], ngz - 1)
         greet_line(plane_sem.at[0], lines[2])
 
-    pl.when(jnp.logical_not(inner))(meet_depth)
+    pl.when(early)(meet_depth)
     tables = [
         weights(h, sizes, (src, disp, mom, perm, phase), (ta, gz), scaling)
         for h in range(lane_rows)
@@ -327,9 +339,12 @@
         carry_link(near, wilson, left, turned, size)
 
         def before(c):
-            if k == nsteps and c == 2:
-                pl.when(jnp.logical_not(inner))(meet_across)
-            sends[k - 1][c].wait_recv()
+            for i, piece in enumerate(PIECES):
+                if c == piece[0]:
+                    if k == nsteps and i == len(PIECES) - 1:
+                        pl.when(outer)(meet_across)
+                    part = far.at[k - 1, :, pl.ds(*piece)]
+                    pltpu.make_async_copy(part, part, s_recv.at[k - 1, i]).wait()
 
         totals.append(pair_sums(far.at[k - 1], left, turned, right, size, before))
 
@@ -345,10 +360,8 @@
         @pl.when((place != root * ngy) & jnp.logical_not(is_served & helped))
         def _():
             give((0, root, 0))
-    @pl.when(inner)
-    def _():
-        meet_depth()
-        meet_across()
+    pl.when(jnp.logical_not(early))(meet_depth)
+    pl.when(inner)(meet_across)
 
     pl.semaphore_wait(plane_sem.at[0], nta - 1)
     each(ranks, place, nroots, give)
@@ -358,15 +371,24 @@
             first = []
             for z in served:
                 slot = z // 2
-                pltpu.make_async_copy(heap.at[z], heap.at[z], heap_recv.at[z]).wait()
-                pltpu.make_async_copy(heap_links.at[slot], heap_links.at[slot], heap_links_recv.at[slot]).wait()
+                both = heap_left.at[slot, pl.ds(0, 3 * size + 9)]
+                pltpu.make_async_copy(both, both, heap_recv.at[slot]).wait()
                 first.append(self_sums(heap.at[z], heap_left.at[slot], heap_turned.at[slot], size))
                 carry_link(heap.at[z], link_at(heap_links.at[slot]), heap_left.at[slot], heap_turned.at[slot], size)
             for z in reversed(served):
                 slot, other = z // 2, (z + 1) % ngz
-                pltpu.make_async_copy(heap.at[other], heap.at[other], heap_recv.at[other]).wait()
+
+                def before(c):
+                    for i, piece in enumerate(PIECES):
+                        if c == 0 == i and slot > 0:
+                            pltpu.make_async_copy(
+                                heap.at[other], heap.at[other], heap_recv.at[len(PIECES) + len(served) + slot - 1]).wait()
+                        if c == piece[0] and slot == 0:
+                            part = heap.at[other, :, pl.ds(*piece)]
+                            pltpu.make_async_copy(part, part, heap_recv.at[len(served) + i]).wait()
+
                 pair = pair_sums(
-                    heap.at[other], heap_left.at[slot], heap_turned.at[slot], right, size, lambda c: None)
+                    heap.at[other], heap_left.at[slot], heap_turned.at[slot], right, size, before)
                 for h in range(lane_rows):
                     gathered[place_of(z), pl.ds(h, 1), :] = row_of(
                         [first[slot], pair], heap_tables[slot, h], tables[h][1])
@@ -461,7 +483,7 @@
         pltpu.VMEM((pairs, 6 * size, sites), jnp.float32),
         pltpu.VMEM((pairs, lane_rows, 32, LANES), jnp.float32),
     ] if helped else []
-    heap_sems = [dma((ngz,)), dma((pairs,))] if helped else []
+    heap_sems = [dma((2 * pairs - 1 + len(PIECES),))] if helped else []
     reduced = pl.pallas_call(
         functools.partial(kernel, sizes, scaling, ranks, helped),
         out_shape=pltpu.VMEM((nta, ndisp * ng * 2, np_), jnp.float32),
@@ -482,7 +504,7 @@
             pltpu.SMEM(gamma_perm.shape, jnp.int32),
             pltpu.SMEM(gamma_phase.shape, jnp.int32),
             pltpu.VMEM((nta * ngz * ngy, lane_rows, LANES), jnp.float32),
-            dma((5,)), dma((1,)), dma((nsteps, 3)),
+            dma((3,)), dma((1,)), dma((nsteps, len(PIECES))),
             dma((1,)), regular((1,)), regular((1,)), regular((1,)),
             *heap_sems,
         ] + [dma((nsteps - 1,))] * (2 if nsteps > 1 else 0),

time: 11.8 us -> 11.7 us (level)
  no operation moved by 1% of the time
where the time goes in v4:
time: 11.7 us; the launch traced here: 11.6 us
  Pallas kernels  11 us (94%)
  local copies, waits for them, and re-layouts  0.61 us (5%)
    pallas_call x1, Pallas kernels, body(): pl.pallas_call(functools.partial(kernel, sizes, scaling, ranks, helped),...  11 us
    unnamed x1, local copies, waits for them, and re-layouts  0.61 us

profile of v4, /device:TPU:0, one launch (start us, length us, event | category | flops | bytes accessed | tf_op | source)
XLA Modules:
  0.0 11.6 jit_solution(17426573863788662198)
XLA Ops:
  0.0 11.0 %shard_map.73 = f32[2,24,4]{2,1,0:T(8,128)S(1)} custom-call(bf16[2,3,48,128]{3,2,1,0:T(8,128)(2,1)} %bitcast.10, bf16[9,2,128]{2,1,0:T(2,128)(2,1)} %bitcast.11, s32[2,4]{1,0:T(2,128)} %refs_2_.1, s32[3]{0:T(128)} %refs_3_.1, s32[4]{0:T(128)} %refs_4_.1, s32[4,4]{1,0:T(4,128)} %refs_5_.1, s32[4,4]{1,0:T(4,128)} %refs_6_.1), custom_call_target="tpu_custom_call" | custom-call | tf_op jit(solution)/shard_map/pallas_call | solution.py:487
  11.0 0.6 %copy.9 = f32[2,3,4,4,2]{3,4,2,1,0:T(2,128)} copy(f32[2,3,4,4,2]{3,4,2,1,0:T(2,128)S(1)} %bitcast.9) | data formatting | bytes 1536

commit v5 on v4

--- a/solution.py
+++ b/solution.py
@@ -74,8 +74,15 @@
 
 
 def site_sums(sums):
-    stacked = jnp.concatenate([jnp.sum(x, axis=0, keepdims=True) for x in sums], axis=0)
-    return jnp.sum(stacked, axis=1, keepdims=True)
+    row = lax.broadcasted_iota(jnp.int32, (8, LANES), 0)
+    for step in (1, 2, 4):
+        first = (row & step) == 0
+        pairs = zip(sums[::2], sums[1::2])
+        sums = [
+            jnp.where(first, x, y) + pltpu.roll(jnp.where(first, y, x), step, 0)
+            for x, y in pairs
+        ]
+    return jnp.sum(jnp.concatenate(sums, axis=0), axis=1, keepdims=True)
 
 
 def keep(left, turned, at, size, real, imag):
@@ -252,37 +259,31 @@
             recv_sem=u_recv.at[k - 1], device_id=target(k), device_id_type=MESH)
         for k in range(1, nsteps)
     ]
+    def to_helper(source, slot, semaphore):
+        pltpu.make_async_remote_copy(
+            src_ref=source, dst_ref=slot, send_sem=s_send.at[0], recv_sem=heap_recv.at[semaphore],
+            device_id=helper_at, device_id_type=MESH).start()
+
+    def field_semaphore(c):
+        slot = lax.rem(gz + ngz - 1, ngz) // 2
+        beyond = jnp.where(slot == 0, c // 2, len(PIECES) + slot - 1)
+        return jnp.where(inner, len(served) + beyond, gz // 2)
+
     for c in range(3):
         loads[c].wait()
         if c == 2:
             loads[3].wait()
         for copies in sends:
             copies[c].start()
-    if helped:
-        def to_helper(source, slot, semaphore):
-            pltpu.make_async_remote_copy(
-                src_ref=source, dst_ref=slot, send_sem=s_send.at[0], recv_sem=semaphore,
-                device_id=helper_at, device_id_type=MESH).start()
-
-        @pl.when(is_served)
-        def _():
-            to_helper(near, heap.at[gz], heap_recv.at[gz // 2])
-
-        @pl.when(is_distant & (gz == served[0] + 1))
-        def _():
-            for i, piece in enumerate(PIECES):
-                to_helper(near.at[:, pl.ds(*piece)], heap.at[gz, :, pl.ds(*piece)], heap_recv.at[len(served) + i])
-
-        @pl.when(is_distant & inner & (gz != served[0] + 1))
-        def _():
-            slot = lax.rem(gz + ngz - 1, ngz) // 2
-            to_helper(near, heap.at[gz], heap_recv.at[len(PIECES) + len(served) + slot - 1])
+        if helped:
+            pl.when(is_distant)(
+                lambda: to_helper(near.at[:, c], heap.at[gz, :, c], field_semaphore(c)))
     for line in lines:
         greet_span(low_sem.at[0], line, 0, line[0])
     if helped:
         @pl.when(is_served)
         def _():
-            to_helper(near_links, heap_links.at[gz // 2], heap_recv.at[gz // 2])
+            to_helper(near_links, heap_links.at[gz // 2], gz // 2)
     for small in smalls:
         small.start()
     for copy in link_sends:

time: 11.7 us -> 11.7 us (level)
  no operation moved by 1% of the time
where the time goes in v5:
time: 11.7 us; the launch traced here: 11.6 us
  Pallas kernels  10.9 us (93%)
  local copies, waits for them, and re-layouts  0.61 us (5%)
    pallas_call x1, Pallas kernels, body(): pl.pallas_call(functools.partial(kernel, sizes, scaling, ranks, helped),...  10.9 us
    unnamed x1, local copies, waits for them, and re-layouts  0.61 us

profile of v5, /device:TPU:0, one launch (start us, length us, event | category | flops | bytes accessed | tf_op | source)
XLA Modules:
  0.0 11.6 jit_solution(11383589109258935484)
XLA Ops:
  0.0 10.9 %shard_map.73 = f32[2,24,4]{2,1,0:T(8,128)S(1)} custom-call(bf16[2,3,48,128]{3,2,1,0:T(8,128)(2,1)} %bitcast.10, bf16[9,2,128]{2,1,0:T(2,128)(2,1)} %bitcast.11, s32[2,4]{1,0:T(2,128)} %refs_2_.1, s32[3]{0:T(128)} %refs_3_.1, s32[4]{0:T(128)} %refs_4_.1, s32[4,4]{1,0:T(4,128)} %refs_5_.1, s32[4,4]{1,0:T(4,128)} %refs_6_.1), custom_call_target="tpu_custom_call" | custom-call | tf_op jit(solution)/shard_map/pallas_call | solution.py:488
  11.0 0.6 %copy.9 = f32[2,3,4,4,2]{3,4,2,1,0:T(2,128)} copy(f32[2,3,4,4,2]{3,4,2,1,0:T(2,128)S(1)} %bitcast.9) | data formatting | bytes 1536

commit v6 on v5

--- a/solution.py
+++ b/solution.py
@@ -259,15 +259,15 @@
             recv_sem=u_recv.at[k - 1], device_id=target(k), device_id_type=MESH)
         for k in range(1, nsteps)
     ]
+
     def to_helper(source, slot, semaphore):
         pltpu.make_async_remote_copy(
             src_ref=source, dst_ref=slot, send_sem=s_send.at[0], recv_sem=heap_recv.at[semaphore],
             device_id=helper_at, device_id_type=MESH).start()
 
     def field_semaphore(c):
-        slot = lax.rem(gz + ngz - 1, ngz) // 2
-        beyond = jnp.where(slot == 0, c // 2, len(PIECES) + slot - 1)
-        return jnp.where(inner, len(served) + beyond, gz // 2)
+        slot = jnp.where(inner, lax.rem(gz + ngz - 1, ngz), gz) // 2
+        return jnp.where(inner & (slot == 0), len(served) + c // 2, slot)
 
     for c in range(3):
         loads[c].wait()
@@ -369,27 +369,27 @@
     if helped:
         @pl.when(is_helper)
         def _():
+            def sides(slot):
+                own = pl.ds(slot * 6 * size, 6 * size)
+                return heap_left.at[own], heap_turned.at[own]
+
             first = []
             for z in served:
                 slot = z // 2
-                both = heap_left.at[slot, pl.ds(0, 3 * size + 9)]
-                pltpu.make_async_copy(both, both, heap_recv.at[slot]).wait()
-                first.append(self_sums(heap.at[z], heap_left.at[slot], heap_turned.at[slot], size))
-                carry_link(heap.at[z], link_at(heap_links.at[slot]), heap_left.at[slot], heap_turned.at[slot], size)
+                bytes_of = heap_left.at[pl.ds(0, (3 if slot == 0 else 6) * size + 9)]
+                pltpu.make_async_copy(bytes_of, bytes_of, heap_recv.at[slot]).wait()
+                first.append(self_sums(heap.at[z], *sides(slot), size))
+                carry_link(heap.at[z], link_at(heap_links.at[slot]), *sides(slot), size)
             for z in reversed(served):
                 slot, other = z // 2, (z + 1) % ngz
 
                 def before(c):
                     for i, piece in enumerate(PIECES):
-                        if c == 0 == i and slot > 0:
-                            pltpu.make_async_copy(
-                                heap.at[other], heap.at[other], heap_recv.at[len(PIECES) + len(served) + slot - 1]).wait()
                         if c == piece[0] and slot == 0:
                             part = heap.at[other, :, pl.ds(*piece)]
                             pltpu.make_async_copy(part, part, heap_recv.at[len(served) + i]).wait()
 
-                pair = pair_sums(
-                    heap.at[other], heap_left.at[slot], heap_turned.at[slot], right, size, before)
+                pair = pair_sums(heap.at[other], *sides(slot), right, size, before)
                 for h in range(lane_rows):
                     gathered[place_of(z), pl.ds(h, 1), :] = row_of(
                         [first[slot], pair], heap_tables[slot, h], tables[h][1])
@@ -401,6 +401,23 @@
             pltpu.make_async_copy(gathered.at[pl.ds(0, rows)], gathered.at[pl.ds(0, rows)], semaphore).wait()
 
     mine = len(served)
+    for copy in link_sends:
+        copy.wait_send()
+    pltpu.make_async_copy(far, far, s_send.at[0]).wait()
+    if helped:
+        @pl.when(is_distant)
+        def _():
+            pltpu.make_async_copy(near, near, s_send.at[0]).wait()
+
+        @pl.when(is_served)
+        def _():
+            pltpu.make_async_copy(near_links, near_links, s_send.at[0]).wait()
+
+        pl.when(is_helper)(lambda: rows_done(s_send.at[0], mine * (nroots - 1)))
+        pl.when(jnp.logical_not(is_served))(lambda: rows_done(s_send.at[0], nroots))
+        rows_done(s_send.at[0], count - 1 - nroots)
+    else:
+        rows_done(s_send.at[0], count - 1)
     if helped:
         pl.when(is_helper)(lambda: rows_done(a_recv.at[0], count - 1 - mine))
         pl.when(jnp.logical_not(is_helper))(lambda: rows_done(a_recv.at[0], count - 1))
@@ -413,23 +430,6 @@
             for row in range(low, min(low + LANES // np_, out.shape[1]), 8):
                 shift = (1 + row - low) * np_
                 out[t, pl.ds(row, 8), :] = pltpu.roll(total, shift, 1, stride=np_, stride_axis=0)[:, :np_]
-    for copy in link_sends:
-        copy.wait_send()
-    pltpu.make_async_copy(far, far, s_send.at[0]).wait()
-    if helped:
-        @pl.when(is_distant)
-        def _():
-            pltpu.make_async_copy(near, near, s_send.at[0]).wait()
-
-        @pl.when(is_served)
-        def _():
-            pltpu.make_async_copy(near_links, near_links, s_send.at[0]).wait()
-
-        pl.when(is_helper)(lambda: rows_done(s_send.at[0], mine * (nroots - 1)))
-        pl.when(jnp.logical_not(is_served))(lambda: rows_done(s_send.at[0], nroots))
-        rows_done(s_send.at[0], count - 1 - nroots)
-    else:
-        rows_done(s_send.at[0], count - 1)
 
 
 def row_sum(ref, start, size, h):
@@ -480,11 +480,11 @@
     heaps = [
         pltpu.VMEM((ngz, 2, 3, size, sites), jnp.bfloat16),
         pltpu.VMEM((pairs, 9, 2, sites), jnp.bfloat16),
-        pltpu.VMEM((pairs, 6 * size, sites), jnp.float32),
-        pltpu.VMEM((pairs, 6 * size, sites), jnp.float32),
+        pltpu.VMEM((pairs * 6 * size, sites), jnp.float32),
+        pltpu.VMEM((pairs * 6 * size, sites), jnp.float32),
         pltpu.VMEM((pairs, lane_rows, 32, LANES), jnp.float32),
     ] if helped else []
-    heap_sems = [dma((2 * pairs - 1 + len(PIECES),))] if helped else []
+    heap_sems = [dma((pairs + len(PIECES),))] if helped else []
     reduced = pl.pallas_call(
         functools.partial(kernel, sizes, scaling, ranks, helped),
         out_shape=pltpu.VMEM((nta, ndisp * ng * 2, np_), jnp.float32),

time: 11.7 us -> 11.7 us (level)
  no operation moved by 1% of the time
where the time goes in v6:
time: 11.7 us; the launch traced here: 11.6 us
  Pallas kernels  10.9 us (93%)
  local copies, waits for them, and re-layouts  0.61 us (5%)
    pallas_call x1, Pallas kernels, body(): pl.pallas_call(functools.partial(kernel, sizes, scaling, ranks, helped),...  10.9 us
    unnamed x1, local copies, waits for them, and re-layouts  0.61 us

profile of v6, /device:TPU:0, one launch (start us, length us, event | category | flops | bytes accessed | tf_op | source)
XLA Modules:
  0.0 11.6 jit_solution(4124918576932592628)
XLA Ops:
  0.0 10.9 %shard_map.73 = f32[2,24,4]{2,1,0:T(8,128)S(1)} custom-call(bf16[2,3,48,128]{3,2,1,0:T(8,128)(2,1)} %bitcast.10, bf16[9,2,128]{2,1,0:T(2,128)(2,1)} %bitcast.11, s32[2,4]{1,0:T(2,128)} %refs_2_.1, s32[3]{0:T(128)} %refs_3_.1, s32[4]{0:T(128)} %refs_4_.1, s32[4,4]{1,0:T(4,128)} %refs_5_.1, s32[4,4]{1,0:T(4,128)} %refs_6_.1), custom_call_target="tpu_custom_call" | custom-call | tf_op jit(solution)/shard_map/pallas_call | solution.py:488
  10.9 0.6 %copy.9 = f32[2,3,4,4,2]{3,4,2,1,0:T(2,128)} copy(f32[2,3,4,4,2]{3,4,2,1,0:T(2,128)S(1)} %bitcast.9) | data formatting | bytes 1536

commit v7 on v6

--- a/solution.py
+++ b/solution.py
@@ -27,8 +27,8 @@
     gamma = (lane // (2 * np_)) & (ng - 1)
     entry = lane // (2 * np_ * ng)
     in_part = row // 16
-    first = (row // 4) & 3
     second = row & 3
+    first = (second - row // 4) & 3
     reach = jnp.full(shape, 2 * nsteps + 1, jnp.int32)
     for j in range(ndisp):
         reach = jnp.where(entry == j, disp[j] - nsteps, reach)
@@ -85,13 +85,28 @@
     return jnp.sum(jnp.concatenate(sums, axis=0), axis=1, keepdims=True)
 
 
+def lane_sums(halves):
+    row = lax.broadcasted_iota(jnp.int32, (8, LANES), 0)
+    folded = [
+        jnp.where(row < 4, x, y) + pltpu.roll(jnp.where(row < 4, y, x), 4, 0)
+        for x, y in zip(halves[::2], halves[1::2])
+    ]
+    return jnp.sum(jnp.concatenate(folded, axis=0), axis=1, keepdims=True)
+
+
+def spins_turned(x, steps):
+    if steps == 0:
+        return x
+    spin = lax.broadcasted_iota(jnp.int32, x.shape, 1) & 3
+    return jnp.where(spin >= steps, pltpu.roll(x, steps, 1), pltpu.roll(x, steps + 4, 1))
+
+
 def keep(left, turned, at, size, real, imag):
     real, imag = real.reshape(-1, LANES), imag.reshape(-1, LANES)
     left[pl.ds(at, size), :] = real
     left[pl.ds(at + size, size), :] = imag
-    if turned is not None:
-        turned[pl.ds(at, size), :] = -imag
-        turned[pl.ds(at + size, size), :] = real
+    turned[pl.ds(at, size), :] = -imag
+    turned[pl.ds(at + size, size), :] = real
 
 
 def self_sums(field, left, turned, size):
@@ -99,7 +114,9 @@
     for c in range(3):
         keep(left, turned, 2 * size * c, size, field[0, c].astype(jnp.float32), field[1, c].astype(jnp.float32))
         sums = add_pairs(sums, left, turned, left, 2 * size * c, 2 * size)
-    return site_sums(sums)
+    return site_sums([
+        sums[16 * side + 4 * ((u - d) % 4) + u] for side in range(2) for d in range(4) for u in range(4)
+    ])
 
 
 def link_at(ref):
@@ -113,7 +130,7 @@
     ]
 
 
-def carry_link(near, wilson, left, turned, size):
+def carry_link(near, wilson, sides, size):
     for chunk in range(size // 16):
         field = [
             [
@@ -125,21 +142,28 @@
         for b in range(3):
             real = sum(field[0][a] * wilson[a][b][0] + field[1][a] * wilson[a][b][1] for a in range(3))
             imag = sum(field[1][a] * wilson[a][b][0] - field[0][a] * wilson[a][b][1] for a in range(3))
-            real, imag = real.reshape(16, LANES), imag.reshape(16, LANES)
-            at = 2 * size * b + chunk * 16
-            left[pl.ds(at, 16), :] = real
-            left[pl.ds(at + size, 16), :] = imag
-            turned[pl.ds(at, 16), :] = -imag
-            turned[pl.ds(at + size, 16), :] = real
-
-
-def pair_sums(far, left, turned, right, size, before):
+            for d in range(4):
+                re = spins_turned(real, d).reshape(16, LANES)
+                im = spins_turned(imag, d).reshape(16, LANES)
+                at = 6 * size * d + 2 * size * b + chunk * 16
+                sides[pl.ds(at, 16), :] = re
+                sides[pl.ds(at + size, 16), :] = im
+                sides[pl.ds(24 * size + at, 16), :] = -im
+                sides[pl.ds(24 * size + at + size, 16), :] = re
+
+
+def pair_sums(far, sides, size, before):
     sums = None
     for c in range(3):
         before(c)
-        keep(right, None, 2 * size * c, size, far[0, c].astype(jnp.float32), far[1, c].astype(jnp.float32))
-        sums = add_pairs(sums, left, turned, right, 2 * size * c, 2 * size)
-    return site_sums(sums)
+        right = jnp.concatenate([far[part, c].astype(jnp.float32) for part in range(2)], axis=0)
+        right = right.reshape(-1, 8, LANES)
+        more = [
+            jnp.sum(sides[pl.ds(6 * size * v + 2 * size * c, 2 * size), :].reshape(-1, 8, LANES) * right, axis=0)
+            for v in range(8)
+        ]
+        sums = more if sums is None else [x + y for x, y in zip(sums, more)]
+    return lane_sums(sums)
 
 
 def row_of(totals, table, reach):
@@ -152,12 +176,12 @@
 def kernel(sizes, scaling, ranks, helped, *refs):
     refs = list(refs)
     prop, links, src_h, disp_h, mom_h, perm_h, phase_h, out = refs[:8]
-    near, near_links, far, far_links, left, turned, right = refs[8:15]
+    near, near_links, far, far_links, left, turned, sides = refs[8:15]
     rest = refs[15:]
-    heap = heap_links = heap_left = heap_turned = heap_tables = None
-    if helped:
-        heap, heap_links, heap_left, heap_turned, heap_tables = rest[:5]
-        rest = rest[5:]
+    heap = heap_links = heap_sides = heap_tables = None
+    if helped:
+        heap, heap_links, heap_sides, heap_tables = rest[:4]
+        rest = rest[4:]
     src, disp, mom, perm, phase, gathered = rest[:6]
     local_sem, s_send, s_recv, a_recv, low_sem, line_sem, plane_sem = rest[6:13]
     rest = rest[13:]
@@ -337,7 +361,7 @@
                 ]
                 for a in range(3)
             ]
-        carry_link(near, wilson, left, turned, size)
+        carry_link(near, wilson, sides, size)
 
         def before(c):
             for i, piece in enumerate(PIECES):
@@ -347,7 +371,7 @@
                     part = far.at[k - 1, :, pl.ds(*piece)]
                     pltpu.make_async_copy(part, part, s_recv.at[k - 1, i]).wait()
 
-        totals.append(pair_sums(far.at[k - 1], left, turned, right, size, before))
+        totals.append(pair_sums(far.at[k - 1], sides, size, before))
 
     for h in range(lane_rows):
         gathered[place, pl.ds(h, 1), :] = row_of(totals, *tables[h])
@@ -369,17 +393,16 @@
     if helped:
         @pl.when(is_helper)
         def _():
-            def sides(slot):
-                own = pl.ds(slot * 6 * size, 6 * size)
-                return heap_left.at[own], heap_turned.at[own]
+            def own(slot):
+                return heap_sides.at[pl.ds(slot * 48 * size, 48 * size)]
 
             first = []
             for z in served:
                 slot = z // 2
-                bytes_of = heap_left.at[pl.ds(0, (3 if slot == 0 else 6) * size + 9)]
+                bytes_of = heap_sides.at[pl.ds(0, (3 if slot == 0 else 6) * size + 9)]
                 pltpu.make_async_copy(bytes_of, bytes_of, heap_recv.at[slot]).wait()
-                first.append(self_sums(heap.at[z], *sides(slot), size))
-                carry_link(heap.at[z], link_at(heap_links.at[slot]), *sides(slot), size)
+                first.append(self_sums(heap.at[z], left, turned, size))
+                carry_link(heap.at[z], link_at(heap_links.at[slot]), own(slot), size)
             for z in reversed(served):
                 slot, other = z // 2, (z + 1) % ngz
 
@@ -389,7 +412,7 @@
                             part = heap.at[other, :, pl.ds(*piece)]
                             pltpu.make_async_copy(part, part, heap_recv.at[len(served) + i]).wait()
 
-                pair = pair_sums(heap.at[other], *sides(slot), right, size, before)
+                pair = pair_sums(heap.at[other], own(slot), size, before)
                 for h in range(lane_rows):
                     gathered[place_of(z), pl.ds(h, 1), :] = row_of(
                         [first[slot], pair], heap_tables[slot, h], tables[h][1])
@@ -480,8 +503,7 @@
     heaps = [
         pltpu.VMEM((ngz, 2, 3, size, sites), jnp.bfloat16),
         pltpu.VMEM((pairs, 9, 2, sites), jnp.bfloat16),
-        pltpu.VMEM((pairs * 6 * size, sites), jnp.float32),
-        pltpu.VMEM((pairs * 6 * size, sites), jnp.float32),
+        pltpu.VMEM((pairs * 48 * size, sites), jnp.float32),
         pltpu.VMEM((pairs, lane_rows, 32, LANES), jnp.float32),
     ] if helped else []
     heap_sems = [dma((pairs + len(PIECES),))] if helped else []
@@ -497,7 +519,7 @@
             pltpu.VMEM((more, 9, 2, sites), jnp.bfloat16),
             pltpu.VMEM((6 * size, sites), jnp.float32),
             pltpu.VMEM((6 * size, sites), jnp.float32),
-            pltpu.VMEM((6 * size, sites), jnp.float32),
+            pltpu.VMEM((48 * size, sites), jnp.float32),
             *heaps,
             pltpu.SMEM(source_z.shape, jnp.int32),
             pltpu.SMEM(displacements.shape, jnp.int32),

time: 11.7 us -> 11.7 us (level)
  no operation moved by 1% of the time
where the time goes in v7:
time: 11.7 us; the launch traced here: 11.5 us
  Pallas kernels  10.9 us (93%)
  local copies, waits for them, and re-layouts  0.61 us (5%)
    pallas_call x1, Pallas kernels, body(): pl.pallas_call(functools.partial(kernel, sizes, scaling, ranks, helped),...  10.9 us
    unnamed x1, local copies, waits for them, and re-layouts  0.61 us

profile of v7, /device:TPU:0, one launch (start us, length us, event | category | flops | bytes accessed | tf_op | source)
XLA Modules:
  0.0 11.5 jit_solution(6387903475404151377)
XLA Ops:
  0.0 10.9 %shard_map.73 = f32[2,24,4]{2,1,0:T(8,128)S(1)} custom-call(bf16[2,3,48,128]{3,2,1,0:T(8,128)(2,1)} %bitcast.10, bf16[9,2,128]{2,1,0:T(2,128)(2,1)} %bitcast.11, s32[2,4]{1,0:T(2,128)} %refs_2_.1, s32[3]{0:T(128)} %refs_3_.1, s32[4]{0:T(128)} %refs_4_.1, s32[4,4]{1,0:T(4,128)} %refs_5_.1, s32[4,4]{1,0:T(4,128)} %refs_6_.1), custom_call_target="tpu_custom_call" | custom-call | tf_op jit(solution)/shard_map/pallas_call | solution.py:510
  10.9 0.6 %copy.9 = f32[2,3,4,4,2]{3,4,2,1,0:T(2,128)} copy(f32[2,3,4,4,2]{3,4,2,1,0:T(2,128)S(1)} %bitcast.9) | data formatting | bytes 1536
